TPU v7x, 32 devices: a whole 2x2x4 slice. The times are simulated.
32 devices in a mesh: ta: 4 (over y, x), gy: 2 (over core), gx: 4 (over z).
Axes of the slice: x: 2, y: 2, z: 4, core: 2. Of those that a mesh axis runs over, the one named last changes fastest.
Arguments:
- features: bfloat16 [16, 4, 416, 192], P('ta', 'gy', 'gx'), may hold values from -6 to 6
- gain_first: float32 [192], replicated, may hold values from 0.1 to 1.9
- kernel_first: bfloat16 [3, 3, 3, 192, 192], replicated, may hold values from -0.078125 to 0.078125
- bias_first: float32 [192], replicated, may hold values from -3 to 3
- gain_second: float32 [192], replicated, may hold values from 0.1 to 1.9
- kernel_second: bfloat16 [3, 3, 3, 192, 192], replicated, may hold values from -0.078125 to 0.078125
- bias_second: float32 [192], replicated, may hold values from -3 to 3
Outputs:
- block_out: bfloat16 [16, 4, 416, 192], P('ta', 'gy', 'gx')
All inputs are finite; a program needn't handle non-finite values.
Results may differ from a plain program's by a relative error of at most 0.0075.
Values may be sent and summed in bfloat16 or wider, within the bound.
A program may use at most 64 MiB of HBM per device.

v0:
```python
import functools

import jax
import jax.numpy as jnp
from jax import lax
from jax.experimental import pallas as pl
from jax.experimental.pallas import tpu as pltpu
from jax.sharding import PartitionSpec as P

epsilon = 1e-06
LATE, EARLY, PAST = 0, 1, 2
TILE = 128
MOVES = [(dy, dx) for dy in (-1, 0, 1) for dx in (-1, 0, 1)]


def moves_of(kind):
    return [m for m in MOVES if (kind == PAST) == (m == (0, 0))]


def activate(field, gain):
    meansq = jnp.mean(field * field, axis=-1, keepdims=True)
    u = field * lax.rsqrt(meansq + epsilon) * gain
    return u / (1.0 + jnp.exp(-u))


def block_kernel(
    feat, gain1, bias1, gain2, bias2, k1, k2, out,
    weights, act, edges, main_out, main_in, row_in, edge_in, line, cols3, acc,
    w_sem, send_sem, recv_sem,
):
    rows, ch, cols = feat.shape[1:]
    colsp = acc.shape[1] // (2 * rows)
    lanes = line.shape[-1]
    ta, gy, gx = (lax.axis_index(a) for a in ("ta", "gy", "gx"))
    n_ta, n_gy, n_gx = (lax.axis_size(a) for a in ("ta", "gy", "gx"))

    def inside(kind, dy, dx, sign):
        t = ta + sign * (1 if kind == PAST else 0)
        y, x = gy + sign * dy, gx + sign * dx
        ok = (t >= 0) & (t < n_ta) & (y >= 0) & (y < n_gy) & (x >= 0) & (x < n_gx)
        return ok, {"ta": t, "gy": y, "gx": x}

    w_copies = [
        pltpu.make_async_copy(k, weights.at[layer, :, pl.ds(0, ch)], w_sem.at[layer])
        for layer, k in enumerate((k1, k2))
    ]
    w_copies[0].start()
    w_copies[1].start()

    barrier = pltpu.get_barrier_semaphore()
    expected = jnp.int32(0)
    for kind in (LATE, PAST):
        for dy, dx in moves_of(kind):
            ok, source = inside(kind, dy, dx, -1)

            @pl.when(ok)
            def _():
                pl.semaphore_signal(
                    barrier, inc=1, device_id=source, device_id_type=pl.DeviceIdType.MESH
                )

            expected = expected + inside(kind, dy, dx, 1)[0].astype(jnp.int32)

    def landing(layer, kind, dy, dx):
        if dx:
            return edge_in.at[layer, kind, dy + 1, (dx + 1) // 2]
        if dy:
            return row_in.at[layer, kind, (dy + 1) // 2]
        return main_in.at[layer]

    def copy_of(layer, kind, dy, dx):
        half = EARLY if kind == EARLY else LATE
        if dx:
            src = edges.at[layer, half, (dx + 1) // 2]
        elif dy:
            src = act.at[layer, half, :, rows - 1 if dy > 0 else 0]
        else:
            src = main_out.at[layer]
        number = kind * 9 + (dy + 1) * 3 + dx + 1
        ok, target = inside(kind, dy, dx, 1)
        return ok, pltpu.make_async_remote_copy(
            src_ref=src,
            dst_ref=landing(layer, kind, dy, dx),
            send_sem=send_sem.at[layer, number],
            recv_sem=recv_sem.at[layer, number],
            device_id=target,
            device_id_type=pl.DeviceIdType.MESH,
        )

    def send(layer, moves):
        for kind, dy, dx in moves:
            ok, copy = copy_of(layer, kind, dy, dx)
            pl.when(ok)(copy.start)

    def send_rim(layer, half):
        send(layer, [(half, *m) for m in sorted(moves_of(half), key=lambda m: (m[1] != 0, m))])

    def receive(layer, kind, moves):
        for dy, dx in moves:
            ok, _ = inside(kind, dy, dx, -1)
            copy = copy_of(layer, kind, dy, dx)[1]
            place = landing(layer, kind, dy, dx)
            pl.when(ok)(copy.wait_recv)

            @pl.when(jnp.logical_not(ok))
            def _():
                place[...] = jnp.zeros_like(place)

    def keep(layer, half, row, values):
        for f, value in enumerate(values):
            packed = value.astype(jnp.bfloat16)
            act[layer, half, f, row] = packed[:, 0:TILE]
            value = packed.astype(jnp.float32)
            at = f * rows + row
            edges[layer, half, 0, at : at + 1, :] = value[0:1]
            edges[layer, half, 1, at : at + 1, :] = value[cols - 1 : cols]
        tails = jnp.concatenate([value[:, TILE:ch] for value in values], axis=1)
        act[layer, half, 2, row] = tails.astype(jnp.bfloat16)

    def spread(layer, kind):
        base = 4 if kind == LATE else 2
        for row in range(-1, rows + 1):
            if row < 0 or row >= rows:
                dy = 1 if row < 0 else -1
                source = row_in.at[layer, kind, (dy + 1) // 2]
                edge_row = rows - 1 if row < 0 else 0
            else:
                dy = 0
                source = act.at[layer, kind, :, row]
                edge_row = row
            tails = source[2].astype(jnp.float32)
            for f in range(2):
                at = f * rows + edge_row
                slot = f * (rows + 2) + row + 1
                line[slot, 8 : 8 + cols, 0:TILE] = source[f].astype(jnp.float32)
                line[slot, 8 : 8 + cols, TILE:lanes] = pltpu.roll(tails, TILE // 2, 1) if f else tails
                line[slot, 7:8, 0:ch] = edge_in[layer, kind, dy + 1, 1, at : at + 1, :]
                line[slot, 8 + cols : 9 + cols, 0:ch] = edge_in[layer, kind, dy + 1, 0, at : at + 1, :]
                for r in range(3):
                    cols3[layer, base + f, row + 1, 0:cols, r * lanes : (r + 1) * lanes] = line[
                        slot, 7 + r : 7 + r + cols, :
                    ].astype(jnp.bfloat16)

    def product(layer, frame, count, p):
        total = None
        for q in range(3):
            piece = cols3[layer, pl.ds(frame, count), q : q + rows].reshape(-1, 3 * lanes)
            kernel = weights[layer, pl.ds(9 * p + 3 * q, 3)].reshape(3 * lanes, ch)
            part = jnp.dot(piece, kernel, preferred_element_type=jnp.float32)
            total = part if total is None else total + part
        return total

    area = rows * colsp

    def convolve_late(layer, own):
        if own:
            acc[1] = product(layer, 4, 2, 2)
        else:
            acc[1] += product(layer, 2, 2, 0) + product(layer, 3, 2, 1)

    def convolve_early(layer):
        acc[0] = product(layer, 2, 2, 2)
        acc[0, area:] += product(layer, 2, 1, 1)

    def hand_on(layer):
        acc[2] = product(layer, 4, 2, 0)
        acc[2, :area] += product(layer, 5, 1, 1)
        for row in range(rows):
            values = [acc[2, pl.ds((f * rows + row) * colsp, cols)] for f in range(2)]
            for f, value in enumerate(values):
                main_out[layer, f, row] = value[:, 0:TILE].astype(jnp.bfloat16)
            tails = jnp.concatenate([value[:, TILE:ch] for value in values], axis=1)
            main_out[layer, 2, row] = tails.astype(jnp.bfloat16)
        send(layer, [(PAST, 0, 0)])

    def add_past(layer):
        receive(layer, PAST, [(0, 0)])
        for row in range(rows):
            tails = main_in[layer, 2, row].astype(jnp.float32)
            for f in range(2):
                at = (f * rows + row) * colsp
                acc[0, at : at + cols, 0:TILE] += main_in[layer, f, row].astype(jnp.float32)
                tail = pltpu.roll(tails, TILE // 2, 1) if f else tails
                acc[0, at : at + cols, TILE:ch] += tail[:, 0 : ch - TILE]

    def cells(half, f, row):
        at = (f * rows + row) * colsp
        return acc[1 - half, at : at + cols, :]

    def middle(half):
        for row in range(rows):
            values = []
            for f in range(2):
                value = (cells(half, f, row) + bias1[...]).astype(jnp.bfloat16).astype(jnp.float32)
                values.append(activate(value, gain2[...]))
            keep(1, half, row, values)

    def finish(half):
        frame = 0 if half == EARLY else 2
        for f in range(2):
            for row in range(rows):
                value = (cells(half, f, row) + bias2[...]).T + feat[frame + f, row].astype(jnp.float32)
                out[frame + f, row] = value.astype(jnp.bfloat16)

    def first(half):
        frame = 0 if half == EARLY else 2
        for row in range(rows):
            keep(0, half, row, [
                activate(feat[frame + f, row].astype(jnp.float32).T, gain1[...]) for f in range(2)
            ])

    edges[...] = jnp.zeros_like(edges)
    first(LATE)
    pl.semaphore_wait(barrier, expected)
    send_rim(0, LATE)
    first(EARLY)
    send_rim(0, EARLY)
    weights[:, :, ch:, :] = jnp.zeros((2, weights.shape[1], lanes - ch, ch), jnp.bfloat16)
    line[...] = jnp.zeros_like(line)
    receive(0, LATE, moves_of(LATE))
    spread(0, LATE)
    w_copies[0].wait()
    hand_on(0)
    receive(0, EARLY, moves_of(EARLY))
    spread(0, EARLY)
    convolve_late(0, True)
    convolve_late(0, False)
    middle(LATE)
    send_rim(1, LATE)
    convolve_early(0)
    w_copies[1].wait()
    receive(1, LATE, moves_of(LATE))
    spread(1, LATE)
    hand_on(1)
    add_past(0)
    middle(EARLY)
    send_rim(1, EARLY)
    convolve_late(1, True)
    receive(1, EARLY, moves_of(EARLY))
    spread(1, EARLY)
    convolve_late(1, False)
    finish(LATE)
    convolve_early(1)
    add_past(1)
    finish(EARLY)
    for layer in range(2):
        for kind in (LATE, EARLY, PAST):
            for dy, dx in moves_of(kind):
                ok, copy = copy_of(layer, kind, dy, dx)
                pl.when(ok)(copy.wait_send)


def local(features, gain_first, kernel_first, bias_first, gain_second, kernel_second, bias_second):
    frames, rows, cols, ch = features.shape
    colsp = -(-cols // 16) * 16
    lanes = -(-ch // 128) * 128
    vmem = pl.BlockSpec(memory_space=pltpu.VMEM)
    hbm = pl.BlockSpec(memory_space=pl.ANY)
    edge_rows = -(-2 * rows // 8) * 8
    bf16, f32 = jnp.bfloat16, jnp.float32
    result = pl.pallas_call(
        block_kernel,
        out_shape=jax.ShapeDtypeStruct((frames, rows, ch, cols), bf16),
        in_specs=[vmem] * 5 + [hbm] * 2,
        out_specs=vmem,
        scratch_shapes=[
            pltpu.VMEM((2, 27, lanes, ch), bf16),
            pltpu.VMEM((2, 2, 3, rows, cols, TILE), bf16),
            pltpu.VMEM((2, 2, 2, edge_rows, ch), f32),
            pltpu.VMEM((2, 3, rows, cols, TILE), bf16),
            pltpu.VMEM((2, 3, rows, cols, TILE), bf16),
            pltpu.VMEM((2, 2, 2, 3, cols, TILE), bf16),
            pltpu.VMEM((2, 2, 3, 2, edge_rows, ch), f32),
            pltpu.VMEM((2 * (rows + 2), cols + 16, lanes), f32),
            pltpu.VMEM((2, frames + 2, rows + 2, colsp, 3 * lanes), bf16),
            pltpu.VMEM((3, 2 * rows * colsp, ch), f32),
            pltpu.SemaphoreType.DMA((2,)),
            pltpu.SemaphoreType.DMA((2, 27)),
            pltpu.SemaphoreType.DMA((2, 27)),
        ],
        compiler_params=pltpu.CompilerParams(
            collective_id=0, has_side_effects=True, vmem_limit_bytes=56 * 1024 * 1024
        ),
        name="residual_block",
    )(
        jnp.swapaxes(features, 2, 3),
        gain_first.reshape(1, ch),
        bias_first.reshape(1, ch),
        gain_second.reshape(1, ch),
        bias_second.reshape(1, ch),
        kernel_first.reshape(27, ch, ch),
        kernel_second.reshape(27, ch, ch),
    )
    return jnp.swapaxes(result, 2, 3)


def solution(mesh):
    placed = (P("ta", "gy", "gx", None), P(), P(), P(), P(), P(), P())
    return jax.shard_map(
        local, mesh=mesh, in_specs=placed, out_specs=P("ta", "gy", "gx", None), check_vma=False
    )
```

profile of v0, /device:TPU:0, one launch (start us, length us, event | category | flops | bytes accessed | tf_op | source)
XLA Modules:
  0.0 25.9 jit_solution(2650408647411177961)
XLA Ops:
  0.0 24.1 %residual_block.1 = bf16[4,2,192,104]{3,2,1,0:T(8,128)(2,1)} custom-call(bf16[4,2,192,104]{3,2,1,0:T(8,128)(2,1)} %bitcast.11, f32[1,192]{1,0:T(1,128)} %bitcast.12, f32[1,192]{1,0:T(1,128)} %bitcast.13, f32[1,192]{1,0:T(1,128)} %bitcast.14, f32[1,192]{1,0:T(1,128)} %bitcast.15, bf16[27,192,192]{2,1,0:T(8,128)(2,1)} %bitcast.8, bf16[27,192,192]{2,1,0:T(8,128)(2,1)} %bitcast.9), custom_call_target="tpu_custom_call" | custom-call | tf_op jit(solution)/shard_map/residual_block/pallas_call | solution.py:261
  24.1 1.8 %copy.9 = bf16[4,2,104,192]{2,3,1,0:T(8,128)(2,1)} copy(bf16[4,2,104,192]{2,3,1,0:T(8,128)(2,1)} %bitcast.10) | data formatting | bytes 638976
where the time goes:
time: 26 us; the launch traced here: 25.9 us
  Pallas kernels  24.1 us (93%)
  local copies, waits for them, and re-layouts  1.77 us (7%)
    pallas_call x1, Pallas kernels, local(): pl.pallas_call(block_kernel, out_shape=jax.ShapeDtypeStruct((frames, rows...  24.1 us
    unnamed x1, local copies, waits for them, and re-layouts  1.77 us

commit v1 on v0

v1 whole, which is shorter than its diff:
```python
import jax
import jax.numpy as jnp
from jax import lax
from jax.experimental import pallas as pl
from jax.experimental.pallas import tpu as pltpu
from jax.sharding import PartitionSpec as P

epsilon = 1e-06
AXES = ("ta", "gy", "gx")
NOW, PAST = 0, 1
PACK = 16
MATMUL = 256


def activate(field, gain):
    meansq = jnp.mean(field * field, axis=0, keepdims=True)
    u = field * lax.rsqrt(meansq + epsilon) * gain
    return u / (1.0 + jnp.exp(-u))


def message_numbers(frames, rows):
    names = [("edge", kind, dy, dx) for kind in (NOW, PAST) for dy in (-1, 0, 1) for dx in (-1, 1)]
    names += [("rows1", side) for side in range(2)]
    names += [("rows2", f, side) for f in range(frames) for side in range(2)]
    names += [("past1", o) for o in range(rows)]
    names += [("past2", i, o) for i in range(2) for o in range(rows)]
    names += [("pass1", side) for side in range(2)]
    names += [("pass2", i, side) for i in range(2) for side in range(2)]
    return {name: n for n, name in enumerate(names)}


def block_kernel(
    feat, gain1, bias1, gain2, bias2, k1, k2, out,
    fin, fout, raw, wt, vec_raw, vec, plane, past, rows_in, edge_out, edge_in, halo, x, zero, acc,
    vec_sem, in_sem, w_sem, out_sem, send_sem, recv_sem,
):
    frames, rows, ch, cols = fin.shape
    lanes = plane.shape[-1]
    bf16, f32 = jnp.bfloat16, jnp.float32
    taps = 9 * ch
    padded = wt.shape[-1]
    groups = ch // PACK
    width = 2 * frames * rows
    per = lanes // width
    number = message_numbers(frames, rows)
    me = {a: lax.axis_index(a) for a in AXES}
    size = {a: lax.axis_size(a) for a in AXES}
    ta, gy, gx = (me[a] for a in AXES)

    def at(dt, dy, dx):
        place = {"ta": ta + dt, "gy": gy + dy, "gx": gx + dx}
        ok = None
        for a, d in zip(AXES, (dt, dy, dx)):
            if isinstance(d, int) and d == 0:
                continue
            inside = (place[a] >= 0) & (place[a] < size[a])
            ok = inside if ok is None else ok & inside
        return ok, place

    moves = [(0, dy, dx) for dy in (-1, 0, 1) for dx in (-1, 0, 1) if dy or dx]
    moves += [(1, 0, 0)] + [(1, dy, dx) for dy in (-1, 0, 1) for dx in (-1, 1)]
    barrier = pltpu.get_barrier_semaphore()
    expected = jnp.int32(0)
    for dt, dy, dx in moves:
        ok, source = at(-dt, -dy, -dx)

        @pl.when(ok)
        def _():
            pl.semaphore_signal(
                barrier, inc=1, device_id=source, device_id_type=pl.DeviceIdType.MESH
            )

        expected = expected + at(dt, dy, dx)[0].astype(jnp.int32)

    fin_copies = [pltpu.make_async_copy(feat.at[f], fin.at[f], in_sem.at[f]) for f in range(frames)]
    for f in reversed(range(frames)):
        fin_copies[f].start()
    vec_copies = [
        pltpu.make_async_copy(v, vec_raw.at[i], vec_sem.at[i])
        for i, v in enumerate((gain1, bias1, gain2, bias2))
    ]
    for copy in vec_copies:
        copy.start()
    w_copies = [
        [
            pltpu.make_async_copy(
                k.at[pl.ds(p * taps, taps)], raw.at[layer, pl.ds(p * taps, taps)], w_sem.at[layer, p]
            )
            for p in range(3)
        ]
        for layer, k in enumerate((k1, k2))
    ]
    for layer in range(2):
        for p in (2, 1, 0):
            w_copies[layer][p].start()

    def copy_to(name, src, dst, target):
        n = number[name] if isinstance(name, tuple) else name
        return pltpu.make_async_remote_copy(
            src_ref=src,
            dst_ref=dst,
            send_sem=send_sem.at[n],
            recv_sem=recv_sem.at[n],
            device_id=target,
            device_id_type=pl.DeviceIdType.MESH,
        )

    def edge_copy(kind, dy, dx):
        side = (dx + 1) // 2
        target = at(kind, dy, dx)[1]
        return copy_to(("edge", kind, dy, dx), edge_out.at[side], edge_in.at[kind, dy + 1, side], target)

    def line(dy):
        return rows - 1 if dy > 0 else 0

    def rows1_copy(side):
        dy = 1 if side == 0 else -1
        src = plane.at[0, :, line(dy)]
        return copy_to(("rows1", side), src, rows_in.at[0, side, pl.ds(2, frames)], at(0, dy, 0)[1])

    def rows2_copy(f, side):
        dy = 1 if side == 0 else -1
        src = plane.at[1, f, line(dy)]
        return copy_to(("rows2", f, side), src, rows_in.at[1, side, 2 + f], at(0, dy, 0)[1])

    def turn(o):
        return jnp.where(gy == 0, rows - 1 - o, o)

    def past1_copy(o):
        r = turn(o)
        src = plane.at[0, pl.ds(frames - 2, 2), r]
        return copy_to(("past1", o), src, past.at[0, :, r], at(1, 0, 0)[1])

    def past2_copy(i, o):
        r = turn(o)
        return copy_to(("past2", i, o), plane.at[1, frames - 2 + i, r], past.at[1, i, r], at(1, 0, 0)[1])

    def pass1_copy(side):
        dy = 1 if side == 0 else -1
        dst = rows_in.at[0, side, pl.ds(0, 2)]
        return copy_to(("pass1", side), past.at[0, :, line(dy)], dst, at(0, dy, 0)[1])

    def pass2_copy(i, side):
        dy = 1 if side == 0 else -1
        dst = rows_in.at[1, side, i]
        return copy_to(("pass2", i, side), past.at[1, i, line(dy)], dst, at(0, dy, 0)[1])

    has_past, has_next = ta > 0, ta < size["ta"] - 1
    from_side = (gy > 0, gy < size["gy"] - 1)
    to_side = (gy < size["gy"] - 1, gy > 0)

    for side in range(2):
        @pl.when(jnp.logical_not(from_side[side]))
        def _():
            rows_in[:, side] = jnp.zeros((2, frames + 2, ch, lanes), bf16)

    @pl.when(jnp.logical_not(has_past))
    def _():
        past[...] = jnp.zeros_like(past)
        rows_in[:, :, 0:2] = jnp.zeros((2, 2, 2, ch, lanes), bf16)

    for kind in (NOW, PAST):
        for dy in (-1, 0, 1):
            for dx in (-1, 1):
                @pl.when(jnp.logical_not(at(-kind, -dy, -dx)[0]))
                def _():
                    edge_in[kind, dy + 1, (dx + 1) // 2] = jnp.zeros(edge_in.shape[3:], bf16)

    plane[0] = jnp.zeros(plane.shape[1:], bf16)
    zero[...] = jnp.zeros_like(zero)
    if padded > taps:
        for layer in range(2):
            for p in range(3):
                wt[layer, p, :, taps:padded] = jnp.zeros((ch, padded - taps), bf16)
    for i, copy in enumerate(vec_copies):
        copy.wait()
        vec[i] = jnp.broadcast_to(vec_raw[i], (lanes, ch)).T

    lane = lax.broadcasted_iota(jnp.int32, (1, lanes), 1)

    for f in reversed(range(frames)):
        fin_copies[f].wait()
        for row in range(rows):
            value = activate(fin[f, row].astype(f32), vec[0, :, 0:cols])
            plane[0, f, row, :, 0:cols] = value.astype(bf16)

    def place(v, shift):
        shift = shift % lanes
        return pltpu.roll(v, shift, 1) if shift else v

    lane_pack = lax.broadcasted_iota(jnp.int32, (PACK, lanes), 1)

    def within(low, count):
        return (lane_pack >= low) & (lane_pack < low + count)

    for side in range(2):
        first_col = 0 if side == 0 else cols - 2
        for b in range(edge_out.shape[1] // PACK):
            total = jnp.zeros((PACK, lanes), bf16)
            for f in range(frames):
                for row in range(rows):
                    slot = 2 * (f * rows + row)
                    for g in range(b * per, min(groups, (b + 1) * per)):
                        low = (g - b * per) * width + slot
                        v = plane[0, f, row, g * PACK : (g + 1) * PACK, :]
                        total = jnp.where(within(low, 2), place(v, low - first_col), total)
            edge_out[side, b * PACK : (b + 1) * PACK, :] = total

    pl.semaphore_wait(barrier, expected)
    for dy in (0, -1, 1):
        for dx in (-1, 1):
            pl.when(at(0, dy, dx)[0])(edge_copy(NOW, dy, dx).start)
    for side in range(2):
        pl.when(to_side[side])(rows1_copy(side).start)

    @pl.when(has_next)
    def _():
        for o in range(rows):
            past1_copy(o).start()

    for dy in (0, -1, 1):
        for dx in (-1, 1):
            pl.when(at(1, dy, dx)[0])(edge_copy(PAST, dy, dx).start)

    def transpose_weights(layer):
        for p in (2, 1, 0):
            w_copies[layer][p].wait()
            for low in range(0, taps, lanes):
                count = min(lanes, taps - low)
                block = raw[layer, p * taps + low : p * taps + low + count, :]
                wt[layer, p, :, low : low + count] = block.T

    transpose_weights(0)
    transpose_weights(1)

    def receive_edges(kind):
        for dy in (-1, 0, 1):
            for dx in (-1, 1):
                pl.when(at(-kind, -dy, -dx)[0])(edge_copy(kind, dy, dx).wait_recv)
        apart = lanes - 2 - cols
        for dy in (-1, 0, 1):
            for g in range(groups):
                b, low = g // per, (g % per) * width
                right = edge_in[kind, dy + 1, 0, b * PACK : (b + 1) * PACK, :]
                left = edge_in[kind, dy + 1, 1, b * PACK : (b + 1) * PACK, :]
                both = jnp.where(within(0, width), place(right, -low), place(left, apart - low))
                halo[kind, dy + 1, g * PACK : (g + 1) * PACK, :] = both

    lane_ch = lax.broadcasted_iota(jnp.int32, (ch, lanes), 1)
    at_halo = ((lane_ch >= cols) & (lane_ch < cols + 2)) | (lane_ch >= lanes - 2)

    def spread(layer, slot):
        for j in range(rows + 2):
            side = 0 if j == 0 else 1
            if j in (0, rows + 1):
                v = rows_in[layer, side, slot]
            elif slot < 2:
                v = past[layer, slot, j - 1]
            else:
                v = plane[layer, slot - 2, j - 1]
            if layer == 0:
                kind = PAST if slot < 2 else NOW
                dy = 1 if j == 0 else -1 if j == rows + 1 else 0
                f = slot + frames - 2 if slot < 2 else slot - 2
                index = 2 * (f * rows + (line(dy) if dy else j - 1))
                v = jnp.where(at_halo, place(halo[kind, dy + 1], cols - index), v)
            low = j * lanes
            x[layer, slot, 0:ch, low : low + lanes] = place(v, 1)
            x[layer, slot, ch : 2 * ch, low : low + lanes] = v
            x[layer, slot, 2 * ch : 3 * ch, low : low + lanes] = place(v, -1)

    def conv(layer, terms):
        left, right = [], []
        for slot, p in terms:
            left.append(wt[layer, p])
            right += [x[layer, slot, :, q * lanes : (q + rows) * lanes] for q in range(3)]
            if padded > taps:
                right.append(zero[...])
        lhs = left[0] if len(left) == 1 else jnp.concatenate(left, axis=1)
        rhs = jnp.concatenate(right, axis=0)
        return jnp.dot(lhs, rhs, preferred_element_type=f32)

    keep = (lane < cols) | ((lane == cols) & (gx < size["gx"] - 1)) | ((lane == lanes - 1) & (gx > 0))

    def middle(f, total):
        for row in range(rows):
            value = total[:, row * lanes : (row + 1) * lanes] + vec[1]
            value = activate(value.astype(bf16).astype(f32), vec[2])
            plane[1, f, row] = jnp.where(keep, value, 0.0).astype(bf16)
        for side in range(2):
            pl.when(to_side[side])(rows2_copy(f, side).start)
        if f >= frames - 2:
            @pl.when(has_next)
            def _():
                for o in range(rows):
                    past2_copy(f - frames + 2, o).start()

    def finish(f, total):
        for row in range(rows):
            value = total[:, row * lanes : row * lanes + cols] + vec[3, :, 0:cols]
            fout[f, row] = (value + fin[f, row].astype(f32)).astype(bf16)
        pltpu.make_async_copy(fout.at[f], out.at[f], out_sem.at[f]).start()

    for side in range(2):
        pl.when(from_side[side])(rows1_copy(side).wait_recv)
    receive_edges(NOW)
    for slot in range(2, frames + 2):
        spread(0, slot)
    for f in range(2, frames):
        middle(f, conv(0, [(f + p, p) for p in range(3)]))

    @pl.when(has_past)
    def _():
        past1_copy(0).wait_recv()
        for side in range(2):
            pl.when(to_side[side] & (turn(0) == line(1 - 2 * side)))(pass1_copy(side).start)
        for o in range(1, rows):
            past1_copy(o).wait_recv()
        for side in range(2):
            pl.when(to_side[side] & (turn(0) != line(1 - 2 * side)))(pass1_copy(side).start)

    acc[0] = conv(0, [(2, 2)])
    acc[1] = conv(0, [(2, 1), (3, 2)])
    for side in range(2):
        pl.when(has_past & from_side[side])(pass1_copy(side).wait_recv)
    receive_edges(PAST)
    for slot in range(2):
        spread(0, slot)
    middle(1, acc[1] + conv(0, [(1, 0)]))
    middle(0, acc[0] + conv(0, [(0, 0), (1, 1)]))

    def receive_rows2(f):
        for side in range(2):
            pl.when(from_side[side])(rows2_copy(f, side).wait_recv)
        spread(1, f + 2)

    for f in range(2, frames):
        receive_rows2(f)
    acc[2] = conv(1, [(4, 2)])
    acc[3] = conv(1, [(4, 1), (5, 2)])

    def pass_on(i):
        @pl.when(has_past)
        def _():
            past2_copy(i, 0).wait_recv()
            for side in range(2):
                pl.when(to_side[side] & (turn(0) == line(1 - 2 * side)))(pass2_copy(i, side).start)
            for o in range(1, rows):
                past2_copy(i, o).wait_recv()
            for side in range(2):
                pl.when(to_side[side] & (turn(0) != line(1 - 2 * side)))(pass2_copy(i, side).start)

    for f in (1, 0):
        receive_rows2(f)
    finish(3, acc[3] + conv(1, [(3, 0)]))
    finish(2, acc[2] + conv(1, [(2, 0), (3, 1)]))
    pass_on(0)
    acc[1] = conv(1, [(2, 1), (3, 2)])
    pass_on(1)
    acc[0] = conv(1, [(2, 2)])
    for i in range(2):
        for side in range(2):
            pl.when(has_past & from_side[side])(pass2_copy(i, side).wait_recv)
        spread(1, i)
    finish(1, acc[1] + conv(1, [(1, 0)]))
    finish(0, acc[0] + conv(1, [(0, 0), (1, 1)]))

    for kind in (NOW, PAST):
        for dy in (-1, 0, 1):
            for dx in (-1, 1):
                pl.when(at(kind, dy, dx)[0])(edge_copy(kind, dy, dx).wait_send)
    for side in range(2):
        @pl.when(to_side[side])
        def _():
            rows1_copy(side).wait_send()
            for f in range(frames):
                rows2_copy(f, side).wait_send()

        @pl.when(to_side[side] & has_past)
        def _():
            pass1_copy(side).wait_send()
            for i in range(2):
                pass2_copy(i, side).wait_send()

    @pl.when(has_next)
    def _():
        for o in range(rows):
            past1_copy(o).wait_send()
            for i in range(2):
                past2_copy(i, o).wait_send()

    for f in range(frames):
        pltpu.make_async_copy(fout.at[f], out.at[f], out_sem.at[f]).wait()


def local(features, gain_first, kernel_first, bias_first, gain_second, kernel_second, bias_second):
    frames, rows, cols, ch = features.shape
    lanes = -(-(cols + 4) // 128) * 128
    padded = -(-9 * ch // MATMUL) * MATMUL
    per = lanes // (2 * frames * rows)
    blocks = -(-(ch // PACK) // per)
    hbm = pl.BlockSpec(memory_space=pl.ANY)
    bf16, f32 = jnp.bfloat16, jnp.float32
    messages = len(message_numbers(frames, rows))
    dma = pltpu.SemaphoreType.DMA
    result = pl.pallas_call(
        block_kernel,
        out_shape=jax.ShapeDtypeStruct((frames, rows, ch, cols), bf16),
        in_specs=[hbm] * 7,
        out_specs=hbm,
        scratch_shapes=[
            pltpu.VMEM((frames, rows, ch, cols), bf16),
            pltpu.VMEM((frames, rows, ch, cols), bf16),
            pltpu.VMEM((2, 27 * ch, ch), bf16),
            pltpu.VMEM((2, 3, ch, padded), bf16),
            pltpu.VMEM((4, 1, ch), f32),
            pltpu.VMEM((4, ch, lanes), f32),
            pltpu.VMEM((2, frames, rows, ch, lanes), bf16),
            pltpu.VMEM((2, 2, rows, ch, lanes), bf16),
            pltpu.VMEM((2, 2, frames + 2, ch, lanes), bf16),
            pltpu.VMEM((2, blocks * PACK, lanes), bf16),
            pltpu.VMEM((2, 3, 2, blocks * PACK, lanes), bf16),
            pltpu.VMEM((2, 3, ch, lanes), bf16),
            pltpu.VMEM((2, frames + 2, 3 * ch, (rows + 2) * lanes), bf16),
            pltpu.VMEM((max(padded - 9 * ch, PACK), rows * lanes), bf16),
            pltpu.VMEM((frames, ch, rows * lanes), f32),
            dma((4,)),
            dma((frames,)),
            dma((2, 3)),
            dma((frames,)),
            dma((messages,)),
            dma((messages,)),
        ],
        compiler_params=pltpu.CompilerParams(
            collective_id=0, has_side_effects=True, vmem_limit_bytes=56 * 1024 * 1024
        ),
        name="residual_block",
    )(
        jnp.swapaxes(features, 2, 3),
        gain_first.reshape(1, ch),
        bias_first.reshape(1, ch),
        gain_second.reshape(1, ch),
        bias_second.reshape(1, ch),
        kernel_first.reshape(27 * ch, ch),
        kernel_second.reshape(27 * ch, ch),
    )
    return jnp.swapaxes(result, 2, 3)


def solution(mesh):
    placed = (P("ta", "gy", "gx", None), P(), P(), P(), P(), P(), P())
    return jax.shard_map(
        local, mesh=mesh, in_specs=placed, out_specs=P("ta", "gy", "gx", None), check_vma=False
    )
```

time: 26 us -> 21.6 us (0.83)
  the two profiles are of different devices: /device:TPU:0 before, /device:TPU:29 now
where the time goes in v1:
time: 21.6 us; the launch traced here: 21.4 us
  Pallas kernels  19.6 us (91%)
  local copies, waits for them, and re-layouts  1.77 us (8%)
    pallas_call x1, Pallas kernels, local(): pl.pallas_call(block_kernel, out_shape=jax.ShapeDtypeStruct((frames, rows...  19.6 us
    unnamed x1, local copies, waits for them, and re-layouts  1.77 us

profile of v1, /device:TPU:29, one launch (start us, length us, event | category | flops | bytes accessed | tf_op | source)
XLA Modules:
  0.0 21.4 jit_solution(1306022217024045993)
XLA Ops:
  0.0 19.6 %residual_block.1 = bf16[4,2,192,104]{3,2,1,0:T(8,128)(2,1)} custom-call(bf16[4,2,192,104]{3,2,1,0:T(8,128)(2,1)} %bitcast.11, f32[1,192]{1,0:T(1,128)} %bitcast.12, f32[1,192]{1,0:T(1,128)} %bitcast.13, f32[1,192]{1,0:T(1,128)} %bitcast.14, f32[1,192]{1,0:T(1,128)} %bitcast.15, bf16[5184,192]{1,0:T(8,128)(2,1)} %bitcast.8, bf16[5184,192]{1,0:T(8,128)(2,1)} %bitcast.9), custom_call_target="tpu_custom_call" | custom-call | tf_op jit(solution)/shard_map/residual_block/pallas_call | solution.py:406
  19.6 1.8 %copy.9 = bf16[4,2,104,192]{2,3,1,0:T(8,128)(2,1)} copy(bf16[4,2,104,192]{2,3,1,0:T(8,128)(2,1)} %bitcast.10) | data formatting | bytes 638976

commit v2 on v1

--- a/solution.py
+++ b/solution.py
@@ -31,14 +31,14 @@
 
 def block_kernel(
     feat, gain1, bias1, gain2, bias2, k1, k2, out,
-    fin, fout, raw, wt, vec_raw, vec, plane, past, rows_in, edge_out, edge_in, halo, x, zero, acc,
-    vec_sem, in_sem, w_sem, out_sem, send_sem, recv_sem,
+    fin, raw, wt, vec_raw, vec, plane, past, rows_in, edge_out, edge_in, halo, x, zero, acc,
+    vec_sem, in_sem, w_sem, send_sem, recv_sem,
 ):
     frames, rows, ch, cols = fin.shape
     lanes = plane.shape[-1]
     bf16, f32 = jnp.bfloat16, jnp.float32
     taps = 9 * ch
-    padded = wt.shape[-1]
+    padded = wt.shape[2] * lanes
     groups = ch // PACK
     width = 2 * frames * rows
     per = lanes // width
@@ -171,7 +171,8 @@
     if padded > taps:
         for layer in range(2):
             for p in range(3):
-                wt[layer, p, :, taps:padded] = jnp.zeros((ch, padded - taps), bf16)
+                for low in range(taps // lanes * lanes, padded, lanes):
+                    wt[layer, p, low // lanes] = jnp.zeros((ch, lanes), bf16)
     for i, copy in enumerate(vec_copies):
         copy.wait()
         vec[i] = jnp.broadcast_to(vec_raw[i], (lanes, ch)).T
@@ -228,7 +229,7 @@
             for low in range(0, taps, lanes):
                 count = min(lanes, taps - low)
                 block = raw[layer, p * taps + low : p * taps + low + count, :]
-                wt[layer, p, :, low : low + count] = block.T
+                wt[layer, p, low // lanes, :, 0:count] = block.T
 
     transpose_weights(0)
     transpose_weights(1)
@@ -249,8 +250,13 @@
     lane_ch = lax.broadcasted_iota(jnp.int32, (ch, lanes), 1)
     at_halo = ((lane_ch >= cols) & (lane_ch < cols + 2)) | (lane_ch >= lanes - 2)
 
-    def spread(layer, slot):
-        for j in range(rows + 2):
+    def shifts(layer, slot, j, v):
+        x[layer, slot, j, 0:ch] = place(v, 1)
+        x[layer, slot, j, ch : 2 * ch] = v
+        x[layer, slot, j, 2 * ch : 3 * ch] = place(v, -1)
+
+    def spread(layer, slot, lines):
+        for j in lines:
             side = 0 if j == 0 else 1
             if j in (0, rows + 1):
                 v = rows_in[layer, side, slot]
@@ -264,19 +270,17 @@
                 f = slot + frames - 2 if slot < 2 else slot - 2
                 index = 2 * (f * rows + (line(dy) if dy else j - 1))
                 v = jnp.where(at_halo, place(halo[kind, dy + 1], cols - index), v)
-            low = j * lanes
-            x[layer, slot, 0:ch, low : low + lanes] = place(v, 1)
-            x[layer, slot, ch : 2 * ch, low : low + lanes] = v
-            x[layer, slot, 2 * ch : 3 * ch, low : low + lanes] = place(v, -1)
+            shifts(layer, slot, j, v)
 
     def conv(layer, terms):
         left, right = [], []
         for slot, p in terms:
-            left.append(wt[layer, p])
-            right += [x[layer, slot, :, q * lanes : (q + rows) * lanes] for q in range(3)]
+            left += [wt[layer, p, c] for c in range(wt.shape[2])]
+            for q in range(3):
+                right.append(jnp.concatenate([x[layer, slot, q + r] for r in range(rows)], axis=1))
             if padded > taps:
                 right.append(zero[...])
-        lhs = left[0] if len(left) == 1 else jnp.concatenate(left, axis=1)
+        lhs = jnp.concatenate(left, axis=1)
         rhs = jnp.concatenate(right, axis=0)
         return jnp.dot(lhs, rhs, preferred_element_type=f32)
 
@@ -286,7 +290,11 @@
         for row in range(rows):
             value = total[:, row * lanes : (row + 1) * lanes] + vec[1]
             value = activate(value.astype(bf16).astype(f32), vec[2])
-            plane[1, f, row] = jnp.where(keep, value, 0.0).astype(bf16)
+            value = jnp.where(keep, value, 0.0).astype(bf16)
+            plane[1, f, row] = value
+            shifts(1, f + 2, row + 1, value)
+
+    def send_middle(f):
         for side in range(2):
             pl.when(to_side[side])(rows2_copy(f, side).start)
         if f >= frames - 2:
@@ -298,70 +306,77 @@
     def finish(f, total):
         for row in range(rows):
             value = total[:, row * lanes : row * lanes + cols] + vec[3, :, 0:cols]
-            fout[f, row] = (value + fin[f, row].astype(f32)).astype(bf16)
-        pltpu.make_async_copy(fout.at[f], out.at[f], out_sem.at[f]).start()
-
+            out[f, row] = (value + fin[f, row].astype(f32)).astype(bf16)
+
+    every = range(rows + 2)
     for side in range(2):
         pl.when(from_side[side])(rows1_copy(side).wait_recv)
     receive_edges(NOW)
-    for slot in range(2, frames + 2):
-        spread(0, slot)
+    for slot in range(2, 5):
+        spread(0, slot, every)
     for f in range(2, frames):
+        if f > 2:
+            spread(0, f + 2, every)
         middle(f, conv(0, [(f + p, p) for p in range(3)]))
-
-    @pl.when(has_past)
-    def _():
-        past1_copy(0).wait_recv()
-        for side in range(2):
-            pl.when(to_side[side] & (turn(0) == line(1 - 2 * side)))(pass1_copy(side).start)
-        for o in range(1, rows):
-            past1_copy(o).wait_recv()
-        for side in range(2):
-            pl.when(to_side[side] & (turn(0) != line(1 - 2 * side)))(pass1_copy(side).start)
-
+        send_middle(f)
+
+    def pass_on(wait, copies):
+        @pl.when(has_past)
+        def _():
+            wait(0)
+            for side in range(2):
+                for copy in copies(side):
+                    pl.when(to_side[side] & (turn(0) == line(1 - 2 * side)))(copy.start)
+
+    def pass_rest(wait, copies):
+        @pl.when(has_past)
+        def _():
+            for o in range(1, rows):
+                wait(o)
+            for side in range(2) if size["gy"] > 2 else ():
+                for copy in copies(side):
+                    pl.when(to_side[side] & (turn(0) != line(1 - 2 * side)))(copy.start)
+
+    wait1 = lambda o: past1_copy(o).wait_recv()
+    pass_on(wait1, lambda side: [pass1_copy(side)])
     acc[0] = conv(0, [(2, 2)])
     acc[1] = conv(0, [(2, 1), (3, 2)])
+    pass_rest(wait1, lambda side: [pass1_copy(side)])
     for side in range(2):
         pl.when(has_past & from_side[side])(pass1_copy(side).wait_recv)
     receive_edges(PAST)
     for slot in range(2):
-        spread(0, slot)
+        spread(0, slot, every)
     middle(1, acc[1] + conv(0, [(1, 0)]))
     middle(0, acc[0] + conv(0, [(0, 0), (1, 1)]))
+    for f in (1, 0):
+        send_middle(f)
 
     def receive_rows2(f):
         for side in range(2):
             pl.when(from_side[side])(rows2_copy(f, side).wait_recv)
-        spread(1, f + 2)
+        spread(1, f + 2, (0, rows + 1))
 
     for f in range(2, frames):
         receive_rows2(f)
     acc[2] = conv(1, [(4, 2)])
     acc[3] = conv(1, [(4, 1), (5, 2)])
 
-    def pass_on(i):
-        @pl.when(has_past)
-        def _():
-            past2_copy(i, 0).wait_recv()
-            for side in range(2):
-                pl.when(to_side[side] & (turn(0) == line(1 - 2 * side)))(pass2_copy(i, side).start)
-            for o in range(1, rows):
-                past2_copy(i, o).wait_recv()
-            for side in range(2):
-                pl.when(to_side[side] & (turn(0) != line(1 - 2 * side)))(pass2_copy(i, side).start)
-
     for f in (1, 0):
         receive_rows2(f)
     finish(3, acc[3] + conv(1, [(3, 0)]))
     finish(2, acc[2] + conv(1, [(2, 0), (3, 1)]))
-    pass_on(0)
+    wait2 = [lambda o, i=i: past2_copy(i, o).wait_recv() for i in range(2)]
+    pass2 = [lambda side, i=i: [pass2_copy(i, side)] for i in range(2)]
+    pass_on(wait2[0], pass2[0])
     acc[1] = conv(1, [(2, 1), (3, 2)])
-    pass_on(1)
     acc[0] = conv(1, [(2, 2)])
+    pass_on(wait2[1], pass2[1])
     for i in range(2):
+        pass_rest(wait2[i], pass2[i])
         for side in range(2):
             pl.when(has_past & from_side[side])(pass2_copy(i, side).wait_recv)
-        spread(1, i)
+        spread(1, i, every)
     finish(1, acc[1] + conv(1, [(1, 0)]))
     finish(0, acc[0] + conv(1, [(0, 0), (1, 1)]))
 
@@ -389,14 +404,12 @@
             for i in range(2):
                 past2_copy(i, o).wait_send()
 
-    for f in range(frames):
-        pltpu.make_async_copy(fout.at[f], out.at[f], out_sem.at[f]).wait()
-
 
 def local(features, gain_first, kernel_first, bias_first, gain_second, kernel_second, bias_second):
     frames, rows, cols, ch = features.shape
     lanes = -(-(cols + 4) // 128) * 128
-    padded = -(-9 * ch // MATMUL) * MATMUL
+    whole = max(MATMUL, lanes)
+    padded = -(-9 * ch // whole) * whole
     per = lanes // (2 * frames * rows)
     blocks = -(-(ch // PACK) // per)
     hbm = pl.BlockSpec(memory_space=pl.ANY)
@@ -405,14 +418,13 @@
     dma = pltpu.SemaphoreType.DMA
     result = pl.pallas_call(
         block_kernel,
-        out_shape=jax.ShapeDtypeStruct((frames, rows, ch, cols), bf16),
+        out_shape=pltpu.VMEM((frames, rows, ch, cols), bf16),
         in_specs=[hbm] * 7,
-        out_specs=hbm,
+        out_specs=pl.BlockSpec(memory_space=pltpu.VMEM),
         scratch_shapes=[
             pltpu.VMEM((frames, rows, ch, cols), bf16),
-            pltpu.VMEM((frames, rows, ch, cols), bf16),
             pltpu.VMEM((2, 27 * ch, ch), bf16),
-            pltpu.VMEM((2, 3, ch, padded), bf16),
+            pltpu.VMEM((2, 3, padded // lanes, ch, lanes), bf16),
             pltpu.VMEM((4, 1, ch), f32),
             pltpu.VMEM((4, ch, lanes), f32),
             pltpu.VMEM((2, frames, rows, ch, lanes), bf16),
@@ -421,13 +433,12 @@
             pltpu.VMEM((2, blocks * PACK, lanes), bf16),
             pltpu.VMEM((2, 3, 2, blocks * PACK, lanes), bf16),
             pltpu.VMEM((2, 3, ch, lanes), bf16),
-            pltpu.VMEM((2, frames + 2, 3 * ch, (rows + 2) * lanes), bf16),
+            pltpu.VMEM((2, frames + 2, rows + 2, 3 * ch, lanes), bf16),
             pltpu.VMEM((max(padded - 9 * ch, PACK), rows * lanes), bf16),
             pltpu.VMEM((frames, ch, rows * lanes), f32),
             dma((4,)),
             dma((frames,)),
             dma((2, 3)),
-            dma((frames,)),
             dma((messages,)),
             dma((messages,)),
         ],

time: 21.6 us -> 19 us (0.88)
  the two profiles are of different devices: /device:TPU:29 before, /device:TPU:13 now
where the time goes in v2:
time: 19 us; the launch traced here: 18.9 us
  Pallas kernels  18.1 us (95%)
  local copies, waits for them, and re-layouts  0.75 us (4%)
    pallas_call x1, Pallas kernels, local(): pl.pallas_call(block_kernel, out_shape=pltpu.VMEM((frames, rows, ch, cols...  18.1 us
    unnamed x1, local copies, waits for them, and re-layouts  0.75 us

profile of v2, /device:TPU:13, one launch (start us, length us, event | category | flops | bytes accessed | tf_op | source)
XLA Modules:
  0.0 18.9 jit_solution(1987841371705297321)
XLA Ops:
  0.0 18.1 %residual_block.1 = bf16[4,2,192,104]{3,2,1,0:T(8,128)(2,1)S(1)} custom-call(bf16[4,2,192,104]{3,2,1,0:T(8,128)(2,1)} %bitcast.11, f32[1,192]{1,0:T(1,128)} %bitcast.12, f32[1,192]{1,0:T(1,128)} %bitcast.13, f32[1,192]{1,0:T(1,128)} %bitcast.14, f32[1,192]{1,0:T(1,128)} %bitcast.15, bf16[5184,192]{1,0:T(8,128)(2,1)} %bitcast.9, bf16[5184,192]{1,0:T(8,128)(2,1)} %bitcast.10), custom_call_target="tpu_custom_call" | custom-call | tf_op jit(solution)/shard_map/residual_block/pallas_call | solution.py:419
  18.1 0.7 %copy.9 = bf16[4,2,104,192]{2,3,1,0:T(8,128)(2,1)} copy(bf16[4,2,104,192]{2,3,1,0:T(8,128)(2,1)S(1)} %bitcast.8) | data formatting | bytes 638976

commit v3 on v2

--- a/solution.py
+++ b/solution.py
@@ -19,7 +19,7 @@
 
 
 def message_numbers(frames, rows):
-    names = [("edge", kind, dy, dx) for kind in (NOW, PAST) for dy in (-1, 0, 1) for dx in (-1, 1)]
+    names = [("edge", dy, dx) for dy in (-1, 0, 1) for dx in (-1, 1)] + [("past_edge",)]
     names += [("rows1", side) for side in range(2)]
     names += [("rows2", f, side) for f in range(frames) for side in range(2)]
     names += [("past1", o) for o in range(rows)]
@@ -58,7 +58,7 @@
         return ok, place
 
     moves = [(0, dy, dx) for dy in (-1, 0, 1) for dx in (-1, 0, 1) if dy or dx]
-    moves += [(1, 0, 0)] + [(1, dy, dx) for dy in (-1, 0, 1) for dx in (-1, 1)]
+    moves += [(1, 0, 0)]
     barrier = pltpu.get_barrier_semaphore()
     expected = jnp.int32(0)
     for dt, dy, dx in moves:
@@ -90,9 +90,6 @@
         ]
         for layer, k in enumerate((k1, k2))
     ]
-    for layer in range(2):
-        for p in (2, 1, 0):
-            w_copies[layer][p].start()
 
     def copy_to(name, src, dst, target):
         n = number[name] if isinstance(name, tuple) else name
@@ -105,10 +102,13 @@
             device_id_type=pl.DeviceIdType.MESH,
         )
 
-    def edge_copy(kind, dy, dx):
+    def edge_copy(dy, dx):
         side = (dx + 1) // 2
-        target = at(kind, dy, dx)[1]
-        return copy_to(("edge", kind, dy, dx), edge_out.at[side], edge_in.at[kind, dy + 1, side], target)
+        target = at(0, dy, dx)[1]
+        return copy_to(("edge", dy, dx), edge_out.at[side], edge_in.at[NOW, dy + 1, side], target)
+
+    def past_edge_copy():
+        return copy_to(("past_edge",), edge_in.at[NOW], edge_in.at[PAST], at(1, 0, 0)[1])
 
     def line(dy):
         return rows - 1 if dy > 0 else 0
@@ -158,13 +158,13 @@
     def _():
         past[...] = jnp.zeros_like(past)
         rows_in[:, :, 0:2] = jnp.zeros((2, 2, 2, ch, lanes), bf16)
-
-    for kind in (NOW, PAST):
-        for dy in (-1, 0, 1):
-            for dx in (-1, 1):
-                @pl.when(jnp.logical_not(at(-kind, -dy, -dx)[0]))
-                def _():
-                    edge_in[kind, dy + 1, (dx + 1) // 2] = jnp.zeros(edge_in.shape[3:], bf16)
+        edge_in[PAST] = jnp.zeros(edge_in.shape[1:], bf16)
+
+    for dy in (-1, 0, 1):
+        for dx in (-1, 1):
+            @pl.when(jnp.logical_not(at(0, -dy, -dx)[0]))
+            def _():
+                edge_in[NOW, dy + 1, (dx + 1) // 2] = jnp.zeros(edge_in.shape[3:], bf16)
 
     plane[0] = jnp.zeros(plane.shape[1:], bf16)
     zero[...] = jnp.zeros_like(zero)
@@ -179,8 +179,11 @@
 
     lane = lax.broadcasted_iota(jnp.int32, (1, lanes), 1)
 
+    for copy in fin_copies:
+        copy.wait()
+    for p in (2, 1, 0):
+        w_copies[0][p].start()
     for f in reversed(range(frames)):
-        fin_copies[f].wait()
         for row in range(rows):
             value = activate(fin[f, row].astype(f32), vec[0, :, 0:cols])
             plane[0, f, row, :, 0:cols] = value.astype(bf16)
@@ -210,7 +213,7 @@
     pl.semaphore_wait(barrier, expected)
     for dy in (0, -1, 1):
         for dx in (-1, 1):
-            pl.when(at(0, dy, dx)[0])(edge_copy(NOW, dy, dx).start)
+            pl.when(at(0, dy, dx)[0])(edge_copy(dy, dx).start)
     for side in range(2):
         pl.when(to_side[side])(rows1_copy(side).start)
 
@@ -219,9 +222,8 @@
         for o in range(rows):
             past1_copy(o).start()
 
-    for dy in (0, -1, 1):
-        for dx in (-1, 1):
-            pl.when(at(1, dy, dx)[0])(edge_copy(PAST, dy, dx).start)
+    for p in (2, 1, 0):
+        w_copies[1][p].start()
 
     def transpose_weights(layer):
         for p in (2, 1, 0):
@@ -235,9 +237,13 @@
     transpose_weights(1)
 
     def receive_edges(kind):
-        for dy in (-1, 0, 1):
-            for dx in (-1, 1):
-                pl.when(at(-kind, -dy, -dx)[0])(edge_copy(kind, dy, dx).wait_recv)
+        if kind == PAST:
+            pl.when(has_past)(past_edge_copy().wait_recv)
+        else:
+            for dy in (-1, 0, 1):
+                for dx in (-1, 1):
+                    pl.when(at(0, -dy, -dx)[0])(edge_copy(dy, dx).wait_recv)
+            pl.when(has_next)(past_edge_copy().start)
         apart = lanes - 2 - cols
         for dy in (-1, 0, 1):
             for g in range(groups):
@@ -312,14 +318,6 @@
     for side in range(2):
         pl.when(from_side[side])(rows1_copy(side).wait_recv)
     receive_edges(NOW)
-    for slot in range(2, 5):
-        spread(0, slot, every)
-    for f in range(2, frames):
-        if f > 2:
-            spread(0, f + 2, every)
-        middle(f, conv(0, [(f + p, p) for p in range(3)]))
-        send_middle(f)
-
     def pass_on(wait, copies):
         @pl.when(has_past)
         def _():
@@ -338,52 +336,63 @@
                     pl.when(to_side[side] & (turn(0) != line(1 - 2 * side)))(copy.start)
 
     wait1 = lambda o: past1_copy(o).wait_recv()
-    pass_on(wait1, lambda side: [pass1_copy(side)])
-    acc[0] = conv(0, [(2, 2)])
-    acc[1] = conv(0, [(2, 1), (3, 2)])
-    pass_rest(wait1, lambda side: [pass1_copy(side)])
+    pass1 = lambda side: [pass1_copy(side)]
+    wait2 = [lambda o, i=i: past2_copy(i, o).wait_recv() for i in range(2)]
+    pass2 = [lambda side, i=i: [pass2_copy(i, side)] for i in range(2)]
+
+    def wait_rows2(f):
+        for side in range(2):
+            pl.when(from_side[side])(rows2_copy(f, side).wait_recv)
+
+    outer = (0, rows + 1)
+    for slot in range(2, 5):
+        spread(0, slot, every)
+    middle(2, conv(0, [(2, 0), (3, 1), (4, 2)]))
+    send_middle(2)
+    pass_on(wait1, pass1)
+    spread(0, 5, every)
+    middle(3, conv(0, [(3, 0), (4, 1), (5, 2)]))
+    send_middle(3)
+    pass_rest(wait1, pass1)
     for side in range(2):
         pl.when(has_past & from_side[side])(pass1_copy(side).wait_recv)
     receive_edges(PAST)
     for slot in range(2):
         spread(0, slot, every)
-    middle(1, acc[1] + conv(0, [(1, 0)]))
-    middle(0, acc[0] + conv(0, [(0, 0), (1, 1)]))
+    middle(1, conv(0, [(3, 2), (2, 1), (1, 0)]))
+    middle(0, conv(0, [(2, 2), (1, 1), (0, 0)]))
     for f in (1, 0):
         send_middle(f)
 
-    def receive_rows2(f):
-        for side in range(2):
-            pl.when(from_side[side])(rows2_copy(f, side).wait_recv)
-        spread(1, f + 2, (0, rows + 1))
-
-    for f in range(2, frames):
-        receive_rows2(f)
+    for f in (2, 3):
+        wait_rows2(f)
+    for slot in (4, 5):
+        spread(1, slot, outer)
+    acc[3] = conv(1, [(4, 1), (5, 2)])
     acc[2] = conv(1, [(4, 2)])
-    acc[3] = conv(1, [(4, 1), (5, 2)])
-
     for f in (1, 0):
-        receive_rows2(f)
+        wait_rows2(f)
+    for slot in (3, 2):
+        spread(1, slot, outer)
+    pass_on(wait2[0], pass2[0])
     finish(3, acc[3] + conv(1, [(3, 0)]))
-    finish(2, acc[2] + conv(1, [(2, 0), (3, 1)]))
-    wait2 = [lambda o, i=i: past2_copy(i, o).wait_recv() for i in range(2)]
-    pass2 = [lambda side, i=i: [pass2_copy(i, side)] for i in range(2)]
-    pass_on(wait2[0], pass2[0])
-    acc[1] = conv(1, [(2, 1), (3, 2)])
+    finish(2, acc[2] + conv(1, [(3, 1), (2, 0)]))
+    pass_on(wait2[1], pass2[1])
+    acc[1] = conv(1, [(3, 2), (2, 1)])
     acc[0] = conv(1, [(2, 2)])
-    pass_on(wait2[1], pass2[1])
     for i in range(2):
         pass_rest(wait2[i], pass2[i])
+    for i in range(2):
         for side in range(2):
             pl.when(has_past & from_side[side])(pass2_copy(i, side).wait_recv)
+    for i in (1, 0):
         spread(1, i, every)
     finish(1, acc[1] + conv(1, [(1, 0)]))
-    finish(0, acc[0] + conv(1, [(0, 0), (1, 1)]))
-
-    for kind in (NOW, PAST):
-        for dy in (-1, 0, 1):
-            for dx in (-1, 1):
-                pl.when(at(kind, dy, dx)[0])(edge_copy(kind, dy, dx).wait_send)
+    finish(0, acc[0] + conv(1, [(1, 1), (0, 0)]))
+
+    for dy in (-1, 0, 1):
+        for dx in (-1, 1):
+            pl.when(at(0, dy, dx)[0])(edge_copy(dy, dx).wait_send)
     for side in range(2):
         @pl.when(to_side[side])
         def _():
@@ -399,6 +408,7 @@
 
     @pl.when(has_next)
     def _():
+        past_edge_copy().wait_send()
         for o in range(rows):
             past1_copy(o).wait_send()
             for i in range(2):

time: 19 us -> 17.5 us (0.921)
  the two profiles are of different devices: /device:TPU:13 before, /device:TPU:29 now
where the time goes in v3:
time: 17.5 us; the launch traced here: 17.3 us
  Pallas kernels  16.5 us (94%)
  local copies, waits for them, and re-layouts  0.75 us (4%)
    pallas_call x1, Pallas kernels, local(): pl.pallas_call(block_kernel, out_shape=pltpu.VMEM((frames, rows, ch, cols...  16.5 us
    unnamed x1, local copies, waits for them, and re-layouts  0.75 us

profile of v3, /device:TPU:29, one launch (start us, length us, event | category | flops | bytes accessed | tf_op | source)
XLA Modules:
  0.0 17.3 jit_solution(135627523357916059)
XLA Ops:
  0.0 16.5 %residual_block.1 = bf16[4,2,192,104]{3,2,1,0:T(8,128)(2,1)S(1)} custom-call(bf16[4,2,192,104]{3,2,1,0:T(8,128)(2,1)} %bitcast.11, f32[1,192]{1,0:T(1,128)} %bitcast.12, f32[1,192]{1,0:T(1,128)} %bitcast.13, f32[1,192]{1,0:T(1,128)} %bitcast.14, f32[1,192]{1,0:T(1,128)} %bitcast.15, bf16[5184,192]{1,0:T(8,128)(2,1)} %bitcast.9, bf16[5184,192]{1,0:T(8,128)(2,1)} %bitcast.10), custom_call_target="tpu_custom_call" | custom-call | tf_op jit(solution)/shard_map/residual_block/pallas_call | solution.py:429
  16.5 0.7 %copy.9 = bf16[4,2,104,192]{2,3,1,0:T(8,128)(2,1)} copy(bf16[4,2,104,192]{2,3,1,0:T(8,128)(2,1)S(1)} %bitcast.8) | data formatting | bytes 638976

commit v4 on v3

--- a/solution.py
+++ b/solution.py
@@ -19,7 +19,8 @@
 
 
 def message_numbers(frames, rows):
-    names = [("edge", dy, dx) for dy in (-1, 0, 1) for dx in (-1, 1)] + [("past_edge",)]
+    names = [("edge", dy, dx) for dy in (-1, 0, 1) for dx in (-1, 1)]
+    names += [("past_edge", dy) for dy in (-1, 0, 1)]
     names += [("rows1", side) for side in range(2)]
     names += [("rows2", f, side) for f in range(frames) for side in range(2)]
     names += [("past1", o) for o in range(rows)]
@@ -107,8 +108,13 @@
         target = at(0, dy, dx)[1]
         return copy_to(("edge", dy, dx), edge_out.at[side], edge_in.at[NOW, dy + 1, side], target)
 
-    def past_edge_copy():
-        return copy_to(("past_edge",), edge_in.at[NOW], edge_in.at[PAST], at(1, 0, 0)[1])
+    def past_edge_copy(dy):
+        src, dst = edge_in.at[NOW, dy + 1], edge_in.at[PAST, dy + 1]
+        return copy_to(("past_edge", dy), src, dst, at(1, 0, 0)[1])
+
+    def past_edges(has, act):
+        for dy in (0, -1, 1):
+            pl.when(has & from_side[0 if dy > 0 else 1] if dy else has)(act(past_edge_copy(dy)))
 
     def line(dy):
         return rows - 1 if dy > 0 else 0
@@ -153,6 +159,7 @@
         @pl.when(jnp.logical_not(from_side[side]))
         def _():
             rows_in[:, side] = jnp.zeros((2, frames + 2, ch, lanes), bf16)
+            edge_in[PAST, 2 - 2 * side] = jnp.zeros(edge_in.shape[2:], bf16)
 
     @pl.when(jnp.logical_not(has_past))
     def _():
@@ -238,12 +245,12 @@
 
     def receive_edges(kind):
         if kind == PAST:
-            pl.when(has_past)(past_edge_copy().wait_recv)
+            past_edges(has_past, lambda copy: copy.wait_recv)
         else:
             for dy in (-1, 0, 1):
                 for dx in (-1, 1):
                     pl.when(at(0, -dy, -dx)[0])(edge_copy(dy, dx).wait_recv)
-            pl.when(has_next)(past_edge_copy().start)
+            past_edges(has_next, lambda copy: copy.start)
         apart = lanes - 2 - cols
         for dy in (-1, 0, 1):
             for g in range(groups):
@@ -256,12 +263,15 @@
     lane_ch = lax.broadcasted_iota(jnp.int32, (ch, lanes), 1)
     at_halo = ((lane_ch >= cols) & (lane_ch < cols + 2)) | (lane_ch >= lanes - 2)
 
-    def shifts(layer, slot, j, v):
-        x[layer, slot, j, 0:ch] = place(v, 1)
-        x[layer, slot, j, ch : 2 * ch] = v
-        x[layer, slot, j, 2 * ch : 3 * ch] = place(v, -1)
-
-    def spread(layer, slot, lines):
+    def shifts(layer, slot, j, values):
+        low, high = j * lanes, (j + len(values)) * lanes
+        for r in range(3):
+            moved = [place(v, 1 - r) for v in values]
+            wide = moved[0] if len(moved) == 1 else jnp.concatenate(moved, axis=1)
+            x[layer, slot, r * ch : (r + 1) * ch, low:high] = wide
+
+    def gather(layer, slot, lines):
+        values = []
         for j in lines:
             side = 0 if j == 0 else 1
             if j in (0, rows + 1):
@@ -276,14 +286,23 @@
                 f = slot + frames - 2 if slot < 2 else slot - 2
                 index = 2 * (f * rows + (line(dy) if dy else j - 1))
                 v = jnp.where(at_halo, place(halo[kind, dy + 1], cols - index), v)
-            shifts(layer, slot, j, v)
+            values.append(v)
+        return values
+
+    def spread(layer, slot, lines):
+        if len(lines) == rows + 2 and rows % 2 == 0:
+            for j in range(0, rows + 2, 2):
+                shifts(layer, slot, j, gather(layer, slot, (j, j + 1)))
+        else:
+            for j in lines:
+                shifts(layer, slot, j, gather(layer, slot, (j,)))
 
     def conv(layer, terms):
         left, right = [], []
         for slot, p in terms:
             left += [wt[layer, p, c] for c in range(wt.shape[2])]
             for q in range(3):
-                right.append(jnp.concatenate([x[layer, slot, q + r] for r in range(rows)], axis=1))
+                right.append(x[layer, slot, :, q * lanes : (q + rows) * lanes])
             if padded > taps:
                 right.append(zero[...])
         lhs = jnp.concatenate(left, axis=1)
@@ -293,12 +312,14 @@
     keep = (lane < cols) | ((lane == cols) & (gx < size["gx"] - 1)) | ((lane == lanes - 1) & (gx > 0))
 
     def middle(f, total):
+        values = []
         for row in range(rows):
             value = total[:, row * lanes : (row + 1) * lanes] + vec[1]
             value = activate(value.astype(bf16).astype(f32), vec[2])
             value = jnp.where(keep, value, 0.0).astype(bf16)
             plane[1, f, row] = value
-            shifts(1, f + 2, row + 1, value)
+            values.append(value)
+        shifts(1, f + 2, 1, values)
 
     def send_middle(f):
         for side in range(2):
@@ -406,9 +427,10 @@
             for i in range(2):
                 pass2_copy(i, side).wait_send()
 
+    past_edges(has_next, lambda copy: copy.wait_send)
+
     @pl.when(has_next)
     def _():
-        past_edge_copy().wait_send()
         for o in range(rows):
             past1_copy(o).wait_send()
             for i in range(2):
@@ -443,7 +465,7 @@
             pltpu.VMEM((2, blocks * PACK, lanes), bf16),
             pltpu.VMEM((2, 3, 2, blocks * PACK, lanes), bf16),
             pltpu.VMEM((2, 3, ch, lanes), bf16),
-            pltpu.VMEM((2, frames + 2, rows + 2, 3 * ch, lanes), bf16),
+            pltpu.VMEM((2, frames + 2, 3 * ch, (rows + 2) * lanes), bf16),
             pltpu.VMEM((max(padded - 9 * ch, PACK), rows * lanes), bf16),
             pltpu.VMEM((frames, ch, rows * lanes), f32),
             dma((4,)),

time: 17.5 us -> 16.9 us (0.966)
  Pallas kernels: 16.5 us -> 15.9 us
    pallas_call x1, Pallas kernels: 16.5 us -> 15.9 us  [local(): pl.pallas_call(block_kernel, out_shape=pltpu.VMEM((frames, rows, ch, cols...]
where the time goes in v4:
time: 16.9 us; the launch traced here: 16.6 us
  Pallas kernels  15.9 us (94%)
  local copies, waits for them, and re-layouts  0.75 us (4%)
    pallas_call x1, Pallas kernels, local(): pl.pallas_call(block_kernel, out_shape=pltpu.VMEM((frames, rows, ch, cols...  15.9 us
    unnamed x1, local copies, waits for them, and re-layouts  0.75 us

profile of v4, /device:TPU:29, one launch (start us, length us, event | category | flops | bytes accessed | tf_op | source)
XLA Modules:
  0.0 16.6 jit_solution(3120064068616085462)
XLA Ops:
  0.0 15.9 %residual_block.1 = bf16[4,2,192,104]{3,2,1,0:T(8,128)(2,1)S(1)} custom-call(bf16[4,2,192,104]{3,2,1,0:T(8,128)(2,1)} %bitcast.11, f32[1,192]{1,0:T(1,128)} %bitcast.12, f32[1,192]{1,0:T(1,128)} %bitcast.13, f32[1,192]{1,0:T(1,128)} %bitcast.14, f32[1,192]{1,0:T(1,128)} %bitcast.15, bf16[5184,192]{1,0:T(8,128)(2,1)} %bitcast.9, bf16[5184,192]{1,0:T(8,128)(2,1)} %bitcast.10), custom_call_target="tpu_custom_call" | custom-call | tf_op jit(solution)/shard_map/residual_block/pallas_call | solution.py:451
  15.9 0.7 %copy.9 = bf16[4,2,104,192]{2,3,1,0:T(8,128)(2,1)} copy(bf16[4,2,104,192]{2,3,1,0:T(8,128)(2,1)S(1)} %bitcast.8) | data formatting | bytes 638976

commit v5 on v4

--- a/solution.py
+++ b/solution.py
@@ -15,7 +15,8 @@
 def activate(field, gain):
     meansq = jnp.mean(field * field, axis=0, keepdims=True)
     u = field * lax.rsqrt(meansq + epsilon) * gain
-    return u / (1.0 + jnp.exp(-u))
+    half = 0.5 * u
+    return half + half * jnp.tanh(half)
 
 
 def message_numbers(frames, rows):
@@ -319,7 +320,9 @@
             value = jnp.where(keep, value, 0.0).astype(bf16)
             plane[1, f, row] = value
             values.append(value)
-        shifts(1, f + 2, 1, values)
+        held[f] = values
+
+    held = {}
 
     def send_middle(f):
         for side in range(2):
@@ -329,6 +332,7 @@
             def _():
                 for o in range(rows):
                     past2_copy(f - frames + 2, o).start()
+        shifts(1, f + 2, 1, held[f])
 
     def finish(f, total):
         for row in range(rows):
@@ -370,10 +374,10 @@
         spread(0, slot, every)
     middle(2, conv(0, [(2, 0), (3, 1), (4, 2)]))
     send_middle(2)
-    pass_on(wait1, pass1)
     spread(0, 5, every)
     middle(3, conv(0, [(3, 0), (4, 1), (5, 2)]))
     send_middle(3)
+    pass_on(wait1, pass1)
     pass_rest(wait1, pass1)
     for side in range(2):
         pl.when(has_past & from_side[side])(pass1_copy(side).wait_recv)
@@ -397,20 +401,14 @@
         spread(1, slot, outer)
     pass_on(wait2[0], pass2[0])
     finish(3, acc[3] + conv(1, [(3, 0)]))
+    pass_on(wait2[1], pass2[1])
     finish(2, acc[2] + conv(1, [(3, 1), (2, 0)]))
-    pass_on(wait2[1], pass2[1])
     acc[1] = conv(1, [(3, 2), (2, 1)])
     acc[0] = conv(1, [(2, 2)])
     for i in range(2):
         pass_rest(wait2[i], pass2[i])
-    for i in range(2):
-        for side in range(2):
-            pl.when(has_past & from_side[side])(pass2_copy(i, side).wait_recv)
     for i in (1, 0):
-        spread(1, i, every)
-    finish(1, acc[1] + conv(1, [(1, 0)]))
-    finish(0, acc[0] + conv(1, [(1, 1), (0, 0)]))
-
+        spread(1, i, range(1, rows + 1))
     for dy in (-1, 0, 1):
         for dx in (-1, 1):
             pl.when(at(0, dy, dx)[0])(edge_copy(dy, dx).wait_send)
@@ -421,11 +419,7 @@
             for f in range(frames):
                 rows2_copy(f, side).wait_send()
 
-        @pl.when(to_side[side] & has_past)
-        def _():
-            pass1_copy(side).wait_send()
-            for i in range(2):
-                pass2_copy(i, side).wait_send()
+        pl.when(to_side[side] & has_past)(pass1_copy(side).wait_send)
 
     past_edges(has_next, lambda copy: copy.wait_send)
 
@@ -435,6 +429,20 @@
             past1_copy(o).wait_send()
             for i in range(2):
                 past2_copy(i, o).wait_send()
+
+    for i in range(2):
+        for side in range(2):
+            pl.when(has_past & from_side[side])(pass2_copy(i, side).wait_recv)
+    for i in (1, 0):
+        spread(1, i, outer)
+    finish(1, acc[1] + conv(1, [(1, 0)]))
+    finish(0, acc[0] + conv(1, [(1, 1), (0, 0)]))
+
+    for side in range(2):
+        @pl.when(to_side[side] & has_past)
+        def _():
+            for i in range(2):
+                pass2_copy(i, side).wait_send()
 
 
 def local(features, gain_first, kernel_first, bias_first, gain_second, kernel_second, bias_second):

time: 16.9 us -> 16.9 us (level)
  no operation moved by 1% of the time
where the time goes in v5:
time: 16.9 us; the launch traced here: 16.7 us
  Pallas kernels  16 us (95%)
  local copies, waits for them, and re-layouts  0.75 us (4%)
    pallas_call x1, Pallas kernels, local(): pl.pallas_call(block_kernel, out_shape=pltpu.VMEM((frames, rows, ch, cols...  16 us
    unnamed x1, local copies, waits for them, and re-layouts  0.75 us

profile of v5, /device:TPU:29, one launch (start us, length us, event | category | flops | bytes accessed | tf_op | source)
XLA Modules:
  0.0 16.7 jit_solution(7316426331019826315)
XLA Ops:
  0.0 16.0 %residual_block.1 = bf16[4,2,192,104]{3,2,1,0:T(8,128)(2,1)S(1)} custom-call(bf16[4,2,192,104]{3,2,1,0:T(8,128)(2,1)} %bitcast.11, f32[1,192]{1,0:T(1,128)} %bitcast.12, f32[1,192]{1,0:T(1,128)} %bitcast.13, f32[1,192]{1,0:T(1,128)} %bitcast.14, f32[1,192]{1,0:T(1,128)} %bitcast.15, bf16[5184,192]{1,0:T(8,128)(2,1)} %bitcast.9, bf16[5184,192]{1,0:T(8,128)(2,1)} %bitcast.10), custom_call_target="tpu_custom_call" | custom-call | tf_op jit(solution)/shard_map/residual_block/pallas_call | solution.py:459
  16.0 0.7 %copy.9 = bf16[4,2,104,192]{2,3,1,0:T(8,128)(2,1)} copy(bf16[4,2,104,192]{2,3,1,0:T(8,128)(2,1)S(1)} %bitcast.8) | data formatting | bytes 638976
